TPU v7x, 32 devices: a whole 2x2x4 slice. The times are simulated.
32 devices in a mesh: dp: 8 (over z, x), tensor: 4 (over y, core).
Axes of the slice: x: 2, y: 2, z: 4, core: 2. Of those that a mesh axis runs over, the one named last changes fastest.
Arguments:
- activations: bfloat16 [16, 128, 4096], P('dp'), may hold values from -6 to 6
- out_grads: bfloat16 [16, 128, 20480], P('dp', None, 'tensor'), may hold values from -0.875 to 0.875
- act_scale: bfloat16 [16, 32], P('dp'), may hold values from 1 to 16
- grad_scale: bfloat16 [16, 1, 20480], P('dp', None, 'tensor'), may hold values from 1 to 72
- moment: float32 [20480, 4096], P(('tensor', 'dp')), may hold values from -0.6 to 0.6
- second: float32 [20480, 4096], P(('tensor', 'dp')), may hold values from 0.1 to 1
- master: float32 [20480, 4096], P(('tensor', 'dp')), may hold values from -0.0625 to 0.0625
Outputs:
- new_moment: float32 [20480, 4096], P(('tensor', 'dp'))
- new_second: float32 [20480, 4096], P(('tensor', 'dp'))
- new_master: float32 [20480, 4096], P(('tensor', 'dp'))
- weights: bfloat16 [20480, 4096], P(('tensor', 'dp'))
All inputs are finite; a program needn't handle non-finite values.
Results may differ from a plain program's by a relative error of at most 0.015.
Values may be sent and summed in bfloat16 or wider, within the bound.
A program may use at most 192 MiB of HBM per device.

v0:
```python
import jax
import jax.numpy as jnp
from jax import lax
from jax.sharding import PartitionSpec as P

FF = 20480
ROWS = 4096
TILE = 128


clip_rms = 1.0
beta_first = 0.9
beta_second = 0.95
learn_rate = 0.003
adam_eps = 1e-08


def widen(act_scale):
    tiles = act_scale.astype(jnp.float32)
    spread = jnp.broadcast_to(tiles[:, :, None], tiles.shape + (TILE,))
    return spread.reshape(tiles.shape[0], tiles.shape[1] * TILE)


def transposed_product(grads_rows, acts_rows):
    return lax.dot_general(
        grads_rows, acts_rows, (((0,), (0,)), ((), ())), preferred_element_type=jnp.float32
    )


def per_device(activations, out_grads, act_scale, grad_scale, moment, second, master):
    owners = lax.axis_size("dp")
    owned = out_grads.shape[2] // owners
    weight_rows = activations.shape[2]
    local_tokens = activations.shape[0] * activations.shape[1]
    acts_deq = (
        (activations.astype(jnp.float32) * widen(act_scale)[:, None, :])
        .astype(jnp.bfloat16)
        .reshape(local_tokens, weight_rows)
    )
    grads_deq = (
        (out_grads.astype(jnp.float32) * grad_scale.astype(jnp.float32))
        .astype(jnp.bfloat16)
        .reshape(local_tokens, out_grads.shape[2])
    )
    moved = lax.all_to_all(grads_deq, "dp", split_axis=1, concat_axis=0, tiled=True)
    piece = lax.all_gather(acts_deq, "dp", axis=0, tiled=True)
    count = piece.shape[0]

    def add_group(group, total):
        offset = (group * local_tokens).astype(jnp.int32)
        acts_group = lax.dynamic_slice_in_dim(piece, offset, local_tokens, 0)
        grads_group = lax.dynamic_slice_in_dim(moved, offset, local_tokens, 0)
        term = transposed_product(grads_group, acts_group)
        rounded = lax.optimization_barrier(term.astype(jnp.bfloat16))
        return total + rounded.astype(jnp.float32)

    grad_owned = lax.fori_loop(
        0, count // local_tokens, add_group, jnp.zeros((owned, weight_rows), jnp.float32)
    )
    squares = lax.psum(jnp.sum(grad_owned * grad_owned), ("dp", "tensor"))
    limit = clip_rms * jnp.sqrt(jnp.float32(FF * ROWS))
    factor = jnp.minimum(1.0, limit / jnp.sqrt(squares))
    clipped = factor * grad_owned
    new_moment = beta_first * moment + (1.0 - beta_first) * clipped
    new_second = beta_second * second + (1.0 - beta_second) * clipped * clipped
    new_master = master - learn_rate * new_moment / (jnp.sqrt(new_second) + adam_eps)
    weights = new_master.astype(jnp.bfloat16)
    return (new_moment, new_second, new_master, weights)


def solution(mesh):
    return jax.shard_map(
        per_device,
        mesh=mesh,
        in_specs=(
            P("dp", None, None),
            P("dp", None, "tensor"),
            P("dp", None),
            P("dp", None, "tensor"),
            P(("tensor", "dp"), None),
            P(("tensor", "dp"), None),
            P(("tensor", "dp"), None),
        ),
        out_specs=(
            P(("tensor", "dp"), None),
            P(("tensor", "dp"), None),
            P(("tensor", "dp"), None),
            P(("tensor", "dp"), None),
        ),
        check_vma=False,
    )
```

profile of v0, /device:TPU:0, one launch (start us, length us, event | category | flops | bytes accessed | tf_op | source)
XLA Modules:
  0.0 516.6 jit_solution(14019932499861952802)
XLA Ops:
  8.0 3.4 multiply_convert_fusion.1
  16.8 7.3 %all-to-all-start = ((bf16[256,8,640]{2,0,1:T(8,128)(2,1)}), bf16[256,8,640]{2,0,1:T(8,128)(2,1)S(1)}, u32[]{:S(2)}, u32[]{:S(2)}) async-start(bf16[256,8,640]{2,0,1:T(8,128)(2,1)} %copy.11), calls=%async_computation | async-start | bytes 5242880 | tf_op jit(solution)/shard_map/all_to_all | solution.py:45
  24.1 121.2 %all-to-all-done = bf16[256,8,640]{2,0,1:T(8,128)(2,1)S(1)} async-done(((bf16[256,8,640]{2,0,1:T(8,128)(2,1)}), bf16[256,8,640]{2,0,1:T(8,128)(2,1)S(1)}, u32[]{:S(2)}, u32[]{:S(2)}) %all-to-all-start) | async-done | bytes 2621472 | tf_op jit(solution)/shard_map/all_to_all | solution.py:45
  145.3 151.2 %all-gather.2.cloned.1.call-done = bf16[2048,4096]{1,0:T(8,128)(2,1)} async-done(((bf16[256,4096]{1,0:T(8,128)(2,1)}), bf16[2048,4096]{1,0:T(8,128)(2,1)}) %all-gather.2.cloned.1.call-update) | async-done | bytes 16777232 | tf_op jit(solution)/shard_map/all_gather | solution.py:46
  296.5 137.7 %while.14 = (s32[]{:T(128)}, f32[640,4096]{1,0:T(8,128)}, bf16[2048,640]{1,0:T(8,128)(2,1)S(1)}, bf16[2048,4096]{1,0:T(8,128)(2,1)}, s32[]{:T(128)}, /*index=5*/s32[]{:T(128)}, s32[]{:T(128)}, s32[]{:T(128)}) while((s32[]{:T(128)}, f32[640,4096]{1,0:T(8,128)}, bf16[2048,640]{1,0:T(8,128)(2,1)S(1)}, bf16[2048,4096]{1,0:T(8,128)(2,1)}, ...), condition=%wide.region_1.0_spmd.clone, body=%wide.region_0.0_spmd.clone.sunk | while | flops 1352663040 | bytes 33883284 | solution.py:57
  296.5 5.5 %convolution_convert_fusion.2 = bf16[640,4096]{1,0:T(8,128)(2,1)} fusion(bf16[2048,4096]{1,0:T(8,128)(2,1)} %get-tuple-element.155, s32[]{:T(128)S(6)} %select_n.10, bf16[2048,640]{1,0:T(8,128)(2,1)S(1)} %get-tuple-element.154), kind=kOutput, calls=%fused_computation.1.clone.1 | convolution fusion | flops 1344798720 | bytes 7668736 | tf_op jit(solution)/shard_map/while/body/eval_jaxpr/dot_general | solution.py:25
  302.0 9.1 %select_add_fusion.2 = f32[640,4096]{1,0:T(8,128)} fusion(f32[640,4096]{1,0:T(8,128)} %get-tuple-element.145, bf16[640,4096]{1,0:T(8,128)(2,1)} %convolution_convert_fusion.2, pred[]{:T(512)S(6)} %compare.3), kind=kLoop, calls=%fused_computation.clone.1 | loop fusion | flops 7864320 | bytes 26214400 | tf_op jit(solution)/shard_map/while/body/eval_jaxpr/add | solution.py:55
  311.1 5.5 %convolution_convert_fusion.2 = bf16[640,4096]{1,0:T(8,128)(2,1)} fusion(bf16[2048,4096]{1,0:T(8,128)(2,1)} %get-tuple-element.155, s32[]{:T(128)S(6)} %select_n.10, bf16[2048,640]{1,0:T(8,128)(2,1)S(1)} %get-tuple-element.154), kind=kOutput, calls=%fused_computation.1.clone.1 | convolution fusion | flops 1344798720 | bytes 7668736 | tf_op jit(solution)/shard_map/while/body/eval_jaxpr/dot_general | solution.py:25
  316.6 12.1 %select_add_fusion.2 = f32[640,4096]{1,0:T(8,128)} fusion(f32[640,4096]{1,0:T(8,128)} %get-tuple-element.145, bf16[640,4096]{1,0:T(8,128)(2,1)} %convolution_convert_fusion.2, pred[]{:T(512)S(6)} %compare.3), kind=kLoop, calls=%fused_computation.clone.1 | loop fusion | flops 7864320 | bytes 26214400 | tf_op jit(solution)/shard_map/while/body/eval_jaxpr/add | solution.py:55
  328.7 5.5 %convolution_convert_fusion.2 = bf16[640,4096]{1,0:T(8,128)(2,1)} fusion(bf16[2048,4096]{1,0:T(8,128)(2,1)} %get-tuple-element.155, s32[]{:T(128)S(6)} %select_n.10, bf16[2048,640]{1,0:T(8,128)(2,1)S(1)} %get-tuple-element.154), kind=kOutput, calls=%fused_computation.1.clone.1 | convolution fusion | flops 1344798720 | bytes 7668736 | tf_op jit(solution)/shard_map/while/body/eval_jaxpr/dot_general | solution.py:25
  334.2 12.1 %select_add_fusion.2 = f32[640,4096]{1,0:T(8,128)} fusion(f32[640,4096]{1,0:T(8,128)} %get-tuple-element.145, bf16[640,4096]{1,0:T(8,128)(2,1)} %convolution_convert_fusion.2, pred[]{:T(512)S(6)} %compare.3), kind=kLoop, calls=%fused_computation.clone.1 | loop fusion | flops 7864320 | bytes 26214400 | tf_op jit(solution)/shard_map/while/body/eval_jaxpr/add | solution.py:55
  346.3 5.5 %convolution_convert_fusion.2 = bf16[640,4096]{1,0:T(8,128)(2,1)} fusion(bf16[2048,4096]{1,0:T(8,128)(2,1)} %get-tuple-element.155, s32[]{:T(128)S(6)} %select_n.10, bf16[2048,640]{1,0:T(8,128)(2,1)S(1)} %get-tuple-element.154), kind=kOutput, calls=%fused_computation.1.clone.1 | convolution fusion | flops 1344798720 | bytes 7668736 | tf_op jit(solution)/shard_map/while/body/eval_jaxpr/dot_general | solution.py:25
  351.8 12.1 %select_add_fusion.2 = f32[640,4096]{1,0:T(8,128)} fusion(f32[640,4096]{1,0:T(8,128)} %get-tuple-element.145, bf16[640,4096]{1,0:T(8,128)(2,1)} %convolution_convert_fusion.2, pred[]{:T(512)S(6)} %compare.3), kind=kLoop, calls=%fused_computation.clone.1 | loop fusion | flops 7864320 | bytes 26214400 | tf_op jit(solution)/shard_map/while/body/eval_jaxpr/add | solution.py:55
  363.9 5.5 %convolution_convert_fusion.2 = bf16[640,4096]{1,0:T(8,128)(2,1)} fusion(bf16[2048,4096]{1,0:T(8,128)(2,1)} %get-tuple-element.155, s32[]{:T(128)S(6)} %select_n.10, bf16[2048,640]{1,0:T(8,128)(2,1)S(1)} %get-tuple-element.154), kind=kOutput, calls=%fused_computation.1.clone.1 | convolution fusion | flops 1344798720 | bytes 7668736 | tf_op jit(solution)/shard_map/while/body/eval_jaxpr/dot_general | solution.py:25
  369.4 12.1 %select_add_fusion.2 = f32[640,4096]{1,0:T(8,128)} fusion(f32[640,4096]{1,0:T(8,128)} %get-tuple-element.145, bf16[640,4096]{1,0:T(8,128)(2,1)} %convolution_convert_fusion.2, pred[]{:T(512)S(6)} %compare.3), kind=kLoop, calls=%fused_computation.clone.1 | loop fusion | flops 7864320 | bytes 26214400 | tf_op jit(solution)/shard_map/while/body/eval_jaxpr/add | solution.py:55
  381.5 5.5 %convolution_convert_fusion.2 = bf16[640,4096]{1,0:T(8,128)(2,1)} fusion(bf16[2048,4096]{1,0:T(8,128)(2,1)} %get-tuple-element.155, s32[]{:T(128)S(6)} %select_n.10, bf16[2048,640]{1,0:T(8,128)(2,1)S(1)} %get-tuple-element.154), kind=kOutput, calls=%fused_computation.1.clone.1 | convolution fusion | flops 1344798720 | bytes 7668736 | tf_op jit(solution)/shard_map/while/body/eval_jaxpr/dot_general | solution.py:25
  387.0 12.1 %select_add_fusion.2 = f32[640,4096]{1,0:T(8,128)} fusion(f32[640,4096]{1,0:T(8,128)} %get-tuple-element.145, bf16[640,4096]{1,0:T(8,128)(2,1)} %convolution_convert_fusion.2, pred[]{:T(512)S(6)} %compare.3), kind=kLoop, calls=%fused_computation.clone.1 | loop fusion | flops 7864320 | bytes 26214400 | tf_op jit(solution)/shard_map/while/body/eval_jaxpr/add | solution.py:55
  399.1 5.5 %convolution_convert_fusion.2 = bf16[640,4096]{1,0:T(8,128)(2,1)} fusion(bf16[2048,4096]{1,0:T(8,128)(2,1)} %get-tuple-element.155, s32[]{:T(128)S(6)} %select_n.10, bf16[2048,640]{1,0:T(8,128)(2,1)S(1)} %get-tuple-element.154), kind=kOutput, calls=%fused_computation.1.clone.1 | convolution fusion | flops 1344798720 | bytes 7668736 | tf_op jit(solution)/shard_map/while/body/eval_jaxpr/dot_general | solution.py:25
  404.6 12.1 %select_add_fusion.2 = f32[640,4096]{1,0:T(8,128)} fusion(f32[640,4096]{1,0:T(8,128)} %get-tuple-element.145, bf16[640,4096]{1,0:T(8,128)(2,1)} %convolution_convert_fusion.2, pred[]{:T(512)S(6)} %compare.3), kind=kLoop, calls=%fused_computation.clone.1 | loop fusion | flops 7864320 | bytes 26214400 | tf_op jit(solution)/shard_map/while/body/eval_jaxpr/add | solution.py:55
  416.7 5.5 %convolution_convert_fusion.2 = bf16[640,4096]{1,0:T(8,128)(2,1)} fusion(bf16[2048,4096]{1,0:T(8,128)(2,1)} %get-tuple-element.155, s32[]{:T(128)S(6)} %select_n.10, bf16[2048,640]{1,0:T(8,128)(2,1)S(1)} %get-tuple-element.154), kind=kOutput, calls=%fused_computation.1.clone.1 | convolution fusion | flops 1344798720 | bytes 7668736 | tf_op jit(solution)/shard_map/while/body/eval_jaxpr/dot_general | solution.py:25
  422.2 12.1 %select_add_fusion.2 = f32[640,4096]{1,0:T(8,128)} fusion(f32[640,4096]{1,0:T(8,128)} %get-tuple-element.145, bf16[640,4096]{1,0:T(8,128)(2,1)} %convolution_convert_fusion.2, pred[]{:T(512)S(6)} %compare.3), kind=kLoop, calls=%fused_computation.clone.1 | loop fusion | flops 7864320 | bytes 26214400 | tf_op jit(solution)/shard_map/while/body/eval_jaxpr/add | solution.py:55
  434.2 7.3 %multiply_reduce_fusion = f32[]{:T(128)} fusion(f32[640,4096]{1,0:T(8,128)} %get-tuple-element.83), kind=kLoop, calls=%fused_computation.9 | loop fusion | flops 5242879 | bytes 10485764 | tf_op jit(solution)/shard_map/reduce_sum | solution.py:60
  441.5 38.6 %psum.7 = f32[]{:T(128)} all-reduce(f32[]{:T(128)} %multiply_reduce_fusion), channel_id=1, replica_groups=mesh['dp'=8,'tensor'=4] {'dp','tensor'}, use_global_device_ids=true, to_apply=%region_3.0 | all-reduce | flops 1 | bytes 8 | tf_op jit(solution)/shard_map/psum | solution.py:60
  480.8 28.9 %fusion.4 = (bf16[640,4096]{1,0:T(8,128)(2,1)}, f32[640,4096]{1,0:T(8,128)}, f32[640,4096]{1,0:T(8,128)}, f32[640,4096]{1,0:T(8,128)}) fusion(f32[640,4096]{1,0:T(8,128)} %param.15, f32[640,4096]{1,0:T(8,128)} %get-tuple-element.83, f32[]{:T(128)S(6)} %min.3, f32[640,4096]{1,0:T(8,128)} %param.14, f32[640,4096]{1,0:T(8,128)} %param.13), kind=kLoop, calls=%fused_computation.15 | loop fusion | flops 34078720 | bytes 78643200 | tf_op jit(solution)/shard_map/convert_element_type | solution.py:67
  (10 shorter events, 6.2 us)
Async XLA Ops:
  7.2 289.4 %all-gather.2.cloned.1.call-start = ((), (), s32[]{:S(2)}) async-start(), calls=%async_computation.1 | async-start | bytes 18874368 | tf_op jit(solution)/shard_map/all_gather | solution.py:46
  16.8 128.5 %all-to-all-start = ((bf16[256,8,640]{2,0,1:T(8,128)(2,1)}), bf16[256,8,640]{2,0,1:T(8,128)(2,1)S(1)}, u32[]{:S(2)}, u32[]{:S(2)}) async-start(bf16[256,8,640]{2,0,1:T(8,128)(2,1)} %copy.11), calls=%async_computation | async-start | bytes 5242880 | tf_op jit(solution)/shard_map/all_to_all | solution.py:45
Sparse Core Ops, SparseCore 0:
  11.5 284.9 all-gather.1
where the time goes:
time: 517 us
  waiting for transfers between devices  272 us (53%)
  other arithmetic  137 us (26%)
  matrix products  44 us (9%)
  blocking collectives  38.6 us (7%)
  between operations  14.8 us (3%)
  starting transfers between devices  7.32 us (1%)
    all_gather x1, waiting for transfers between devices, per_device(): piece = lax.all_gather(acts_deq, 'dp', axis=0, tiled=True)  151 us
    all_to_all x1, waiting for transfers between devices, per_device(): lax.all_to_all(grads_deq, 'dp', split_axis=1, concat_axis=0, tiled=True)  121 us
    add x8, other arithmetic, add_group(): return total + rounded.astype(jnp.float32)  93.7 us
    dot_general x8, matrix products, transposed_product(): lax.dot_general(grads_rows, acts_rows, (((0,), (0,)), ((), ())), preferre...  44 us
    psum x1, blocking collectives, per_device(): squares = lax.psum(jnp.sum(grad_owned * grad_owned), ('dp', 'tensor'))  38.6 us
    convert_element_type x1, other arithmetic, per_device(): weights = new_master.astype(jnp.bfloat16)  28.9 us
  transfers between devices with their start and end apart: 2, of which 2 were waited for; matrix products, arithmetic and copies ran while one was open for 1% of the time, Pallas kernels for 0%

commit v1 on v0

v1 whole, which is shorter than its diff:
```python
import functools
import math

import jax
import jax.numpy as jnp
from jax import lax
from jax.experimental import pallas as pl
from jax.experimental.pallas import tpu as pltpu
from jax.sharding import PartitionSpec as P

MESH = pl.DeviceIdType.MESH
PAIR = 2

clip_rms = 1.0
beta_first = 0.9
beta_second = 0.95
learn_rate = 0.003
adam_eps = 1e-08


def gather_kernel(
    owners, lanes, acts, grads, full, moved, z_sem, x_sem, y_sem, c_sem, f_sem,
    g_send, own_sem, a_recv, g_recv,
):
    chain = owners // PAIR
    d = lax.axis_index("dp")
    t = lax.axis_index("tensor")
    g, b = d // PAIR, d % PAIR
    y, c = t // PAIR, t % PAIR
    x_dev = (g * PAIR + (1 - b), t)
    y_dev = (d, (1 - y) * PAIR + c)
    c_dev = (d, y * PAIR + (1 - c))
    across = (1 - y) * PAIR + c

    barrier = pltpu.get_barrier_semaphore()
    for o in range(1, owners):
        peer = (lax.rem(d + o, owners), t)
        pl.semaphore_signal(barrier, inc=1, device_id=peer, device_id_type=MESH)
    for peer in (y_dev, c_dev):
        pl.semaphore_signal(barrier, inc=1, device_id=peer, device_id_type=MESH)
    pl.semaphore_wait(barrier, owners + 1)

    def copy(src, slot, send, dev):
        return pltpu.make_async_remote_copy(
            src_ref=src, dst_ref=full.at[slot], send_sem=send, recv_sem=a_recv.at[slot],
            device_id=dev, device_id_type=MESH,
        )

    def held(s, q):
        return full.at[q * owners + s]

    def z_copy(s, up, src):
        to = g + 1 if up else g - 1
        return copy(src, t * owners + s, z_sem.at[up, s], (to * PAIR + b, t))

    def x_copy(s, src):
        return copy(src, t * owners + s, x_sem.at[s], x_dev)

    def y_copy(s):
        return copy(held(s, t), t * owners + s, y_sem.at[s], y_dev)

    def c_copy(s):
        return copy(held(s, t), t * owners + s, c_sem.at[s], c_dev)

    def f_copy(s):
        return copy(held(s, across), across * owners + s, f_sem.at[s], c_dev)

    def got(s, q):
        ref = held(s, q)
        pltpu.make_async_copy(ref, ref, a_recv.at[q * owners + s]).wait()

    def g_copy(o):
        to = lax.rem(d + o, owners)
        return pltpu.make_async_remote_copy(
            src_ref=grads.at[to], dst_ref=moved.at[d], send_sem=g_send.at[o],
            recv_sem=g_recv.at[d], device_id=(to, t), device_id_type=MESH,
        )

    mine = acts.at[t]

    @pl.when(g + 1 < chain)
    def _():
        z_copy(d, 1, mine).start()

    @pl.when(g > 0)
    def _():
        z_copy(d, 0, mine).start()

    x_copy(d, mine).start()
    own = [pltpu.make_async_copy(acts.at[q], held(d, q), own_sem.at[q]) for q in range(lanes)]
    own.append(pltpu.make_async_copy(grads.at[d], moved.at[d], own_sem.at[lanes]))
    for one in own:
        one.start()

    def below(k, act):
        pl.when(g - k >= 0)(lambda: act(g - k, 1))

    def above(k, act):
        pl.when(g + k < chain)(lambda: act(g + k, 0))

    def from_chain(at, up):
        s = at * PAIR + b
        got(s, t)
        onward = (g + 1 < chain) if up else (g > 0)
        pl.when(onward)(lambda: z_copy(s, up, held(s, t)).start())
        x_copy(s, held(s, t)).start()
        y_copy(s).start()
        c_copy(s).start()

    def from_pair(at, up):
        s = at * PAIR + (1 - b)
        got(s, t)
        y_copy(s).start()
        c_copy(s).start()

    def across_chain(at, up):
        s = at * PAIR + b
        got(s, across)
        f_copy(s).start()

    def across_pair(at, up):
        s = at * PAIR + (1 - b)
        got(s, across)
        f_copy(s).start()

    def ends(k, act):
        below(k, act)
        if k > 0:
            above(k, act)

    order = sorted(range(1, owners), key=lambda o: (abs(o - owners // 2), o))
    from_pair(g, 0)
    for k in range(1, chain):
        ends(k, from_chain)
        if k == min(2, chain - 1):
            for o in order:
                g_copy(o).start()
        if k > 1:
            ends(k - 1, from_pair)
        if k == 2:
            across_pair(g, 0)
        if k > 2:
            ends(k - 2, across_chain)
            ends(k - 2, across_pair)
    if chain > 1:
        ends(chain - 1, from_pair)
    if chain <= 2:
        across_pair(g, 0)
    for k in range(max(1, chain - 2), chain):
        ends(k, across_chain)
        ends(k, across_pair)

    for one in own:
        one.wait()
    for o in order:
        s = lax.rem(d + owners - o, owners)
        pltpu.make_async_copy(moved.at[s], moved.at[s], g_recv.at[s]).wait()
    beside = y * PAIR + (1 - c)
    corner = (1 - y) * PAIR + (1 - c)
    for o in range(1, owners):
        s = lax.rem(d + o, owners)
        got(s, beside)
        got(s, corner)

    for o in order:
        g_copy(o).wait_send()
    for o in range(1, owners):
        s = lax.rem(d + o, owners)
        y_copy(s).wait_send()
        c_copy(s).wait_send()
        f_copy(s).wait_send()
    x_copy(d, mine).wait_send()
    pl.when(g + 1 < chain)(lambda: z_copy(d, 1, mine).wait_send())
    pl.when(g > 0)(lambda: z_copy(d, 0, mine).wait_send())

    def chain_sent(at, up):
        s = at * PAIR + b
        onward = (g + 1 < chain) if up else (g > 0)
        pl.when(onward)(lambda: z_copy(s, up, held(s, t)).wait_send())
        x_copy(s, held(s, t)).wait_send()

    for k in range(1, chain):
        ends(k, chain_sent)


def gather_all(acts, grads, owners):
    lanes, tokens, quarter = acts.shape
    dma = pltpu.SemaphoreType.DMA
    return pl.pallas_call(
        functools.partial(gather_kernel, owners, lanes),
        out_shape=(
            jax.ShapeDtypeStruct((lanes * owners, tokens, quarter), acts.dtype),
            jax.ShapeDtypeStruct(grads.shape, grads.dtype),
        ),
        in_specs=[pl.BlockSpec(memory_space=pltpu.VMEM)] * 2,
        out_specs=(pl.BlockSpec(memory_space=pl.ANY),) * 2,
        scratch_shapes=[
            dma((2, owners)), dma((owners,)), dma((owners,)), dma((owners,)), dma((owners,)),
            dma((owners,)), dma((lanes + 1,)), dma((lanes * owners,)), dma((owners,)),
        ],
        compiler_params=pltpu.CompilerParams(collective_id=0, has_side_effects=True),
    )(acts, grads)


def norm_kernel(owners, lanes, limit, part, factor, near, far, own_sem, n_send, n_recv, f_send, f_recv):
    d = lax.axis_index("dp")
    t = lax.axis_index("tensor")
    barrier = pltpu.get_barrier_semaphore()
    for o in range(1, lanes):
        peer = (d, lax.rem(t + o, lanes))
        pl.semaphore_signal(barrier, inc=1, device_id=peer, device_id_type=MESH)
    for o in range(1, owners):
        peer = (lax.rem(d + o, owners), t)
        pl.semaphore_signal(barrier, inc=1, device_id=peer, device_id_type=MESH)
    pl.semaphore_wait(barrier, lanes + owners - 2)

    def near_copy(o):
        return pltpu.make_async_remote_copy(
            src_ref=part, dst_ref=near.at[t], send_sem=n_send.at[o], recv_sem=n_recv.at[t],
            device_id=(d, lax.rem(t + o, lanes)), device_id_type=MESH,
        )

    def far_copy(o):
        return pltpu.make_async_remote_copy(
            src_ref=near, dst_ref=far.at[d], send_sem=f_send.at[o], recv_sem=f_recv.at[d],
            device_id=(lax.rem(d + o, owners), t), device_id_type=MESH,
        )

    def got(ref, sem):
        pltpu.make_async_copy(ref, ref, sem).wait()

    for o in range(1, lanes):
        near_copy(o).start()
    own = pltpu.make_async_copy(part, near.at[t], own_sem)
    own.start()
    own.wait()
    for o in range(1, lanes):
        s = lax.rem(t + o, lanes)
        got(near.at[s], n_recv.at[s])
    for o in range(1, owners):
        far_copy(o).start()
    total = jnp.sum(near[...], axis=0)
    for o in range(1, owners):
        s = lax.rem(d + o, owners)
        got(far.at[s], f_recv.at[s])
        total += jnp.sum(far[s], axis=0)
    squares = jnp.sum(total, axis=(0, 1), keepdims=True)
    scale = jnp.minimum(1.0, limit / jnp.sqrt(squares))
    factor[...] = jnp.broadcast_to(scale, factor.shape)
    for o in range(1, lanes):
        near_copy(o).wait_send()
    for o in range(1, owners):
        far_copy(o).wait_send()


def clip_factor(part, owners, lanes, limit):
    dma = pltpu.SemaphoreType.DMA
    return pl.pallas_call(
        functools.partial(norm_kernel, owners, lanes, limit),
        out_shape=jax.ShapeDtypeStruct(part.shape, part.dtype),
        in_specs=[pl.BlockSpec(memory_space=pltpu.VMEM)],
        out_specs=pl.BlockSpec(memory_space=pltpu.VMEM),
        scratch_shapes=[
            pltpu.VMEM((lanes,) + part.shape, part.dtype),
            pltpu.VMEM((owners, lanes) + part.shape, part.dtype),
            dma, dma((lanes,)), dma((lanes,)), dma((owners,)), dma((owners,)),
        ],
        compiler_params=pltpu.CompilerParams(
            collective_id=1, has_side_effects=True, vmem_limit_bytes=4 * 1024 * 1024
        ),
    )(part)


def per_device(activations, out_grads, act_scale, grad_scale, moment, second, master):
    owners = lax.axis_size("dp")
    lanes = lax.axis_size("tensor")
    blocks, tile_tokens, weight_rows = activations.shape
    tiles = act_scale.shape[1]
    local_tokens = blocks * tile_tokens
    columns = out_grads.shape[2]
    owned = columns // owners
    entries = columns * lanes * weight_rows
    quarter = weight_rows // lanes
    spread = jnp.broadcast_to(
        act_scale.astype(jnp.float32)[:, :, None], (blocks, tiles, weight_rows // tiles)
    ).reshape(blocks, 1, weight_rows)
    acts_deq = (activations.astype(jnp.float32) * spread).astype(jnp.bfloat16)
    acts_deq = acts_deq.reshape(local_tokens, lanes, quarter).transpose(1, 0, 2)
    grads_deq = (out_grads.astype(jnp.float32) * grad_scale.astype(jnp.float32)).astype(jnp.bfloat16)
    grads_deq = grads_deq.reshape(local_tokens, owners, owned).transpose(1, 0, 2)
    piece, moved = gather_all(acts_deq, grads_deq, owners)
    total = owners * local_tokens
    moved = moved.reshape(total, owned)
    piece = piece.reshape(lanes, total, quarter)
    parts = []
    for t in range(lanes):
        parts.append(
            lax.dot_general(
                moved, piece[t], (((0,), (0,)), ((), ())), preferred_element_type=jnp.float32
            )
        )
    grad_owned = jnp.concatenate(parts, axis=1)
    part = jnp.sum((grad_owned * grad_owned).reshape(owned // 8, 8, weight_rows // 128, 128), axis=(0, 2))
    limit = clip_rms * math.sqrt(entries)
    factor = clip_factor(part, owners, lanes, limit)[0, 0]
    clipped = factor * grad_owned
    new_moment = beta_first * moment + (1.0 - beta_first) * clipped
    new_second = beta_second * second + (1.0 - beta_second) * clipped * clipped
    new_master = master - learn_rate * new_moment / (jnp.sqrt(new_second) + adam_eps)
    weights = new_master.astype(jnp.bfloat16)
    return (new_moment, new_second, new_master, weights)


def solution(mesh):
    return jax.shard_map(
        per_device,
        mesh=mesh,
        in_specs=(
            P("dp", None, None),
            P("dp", None, "tensor"),
            P("dp", None),
            P("dp", None, "tensor"),
            P(("tensor", "dp"), None),
            P(("tensor", "dp"), None),
            P(("tensor", "dp"), None),
        ),
        out_specs=(
            P(("tensor", "dp"), None),
            P(("tensor", "dp"), None),
            P(("tensor", "dp"), None),
            P(("tensor", "dp"), None),
        ),
        check_vma=False,
    )
```

time: 517 us -> 172 us (0.33)
  waiting for transfers between devices: 272 us -> 0 us
  Pallas kernels: 0 us -> 113 us
  other arithmetic: 137 us -> 31.3 us
  blocking collectives: 38.6 us -> 0 us
  matrix products: 44 us -> 16.7 us
  between operations: 14.8 us -> 0.82 us
  starting transfers between devices: 7.32 us -> 0 us
  local copies, waits for them, and re-layouts: 2.41 us -> 9.41 us
    all_gather x1 -> x0, waiting for transfers between devices: 151 us -> none  [per_device(): piece = lax.all_gather(acts_deq, 'dp', axis=0, tiled=True)]
    all_to_all x1 -> x0, waiting for transfers between devices: 121 us -> none  [per_device(): lax.all_to_all(grads_deq, 'dp', split_axis=1, concat_axis=0, tiled=True)]
    pallas_call x0 -> x2, Pallas kernels: none -> 113 us  [the longest x1 104 us: gather_all(): pl.pallas_call(functools.partial(gather_kernel, owners, lanes), out_shape...]
    add x8 -> x0, other arithmetic: 93.7 us -> none  [add_group(): return total + rounded.astype(jnp.float32)]
    psum x1 -> x0, blocking collectives: 38.6 us -> none  [per_device(): squares = lax.psum(jnp.sum(grad_owned * grad_owned), ('dp', 'tensor'))]
    dot_general x8 -> x4, matrix products: 44 us -> 16.7 us  [per_device(): lax.dot_general(moved, piece[t], (((0,), (0,)), ((), ())), preferred_elem...]
    reshape x0 -> x3, local copies, waits for them, and re-layouts: none -> 8.27 us  [the longest x2 6.45 us: per_device(): acts_deq = acts_deq.reshape(local_tokens, lanes, quarter).transpose(1, 0, 2)]
    all_to_all x1 -> x0, starting transfers between devices: 7.28 us -> none  [per_device(): lax.all_to_all(grads_deq, 'dp', split_axis=1, concat_axis=0, tiled=True)]
  transfers between devices with their start and end apart: 2 -> 0, of which waited for: 2 -> 0; matrix products, arithmetic and copies ran while one was open for 1% -> 0% of each run, Pallas kernels for 0% -> 0%
where the time goes in v1:
time: 172 us; the launch traced here: 171 us
  Pallas kernels  113 us (66%)
  other arithmetic  31.3 us (18%)
  matrix products  16.7 us (10%)
  local copies, waits for them, and re-layouts  9.41 us (5%)
    pallas_call x1, Pallas kernels, gather_all(): pl.pallas_call(functools.partial(gather_kernel, owners, lanes), out_shape...  104 us
    convert_element_type x1, other arithmetic, per_device(): weights = new_master.astype(jnp.bfloat16)  24.5 us
    dot_general x4, matrix products, per_device(): lax.dot_general(moved, piece[t], (((0,), (0,)), ((), ())), preferred_elem...  16.7 us
    pallas_call x1, Pallas kernels, clip_factor(): pl.pallas_call(functools.partial(norm_kernel, owners, lanes, limit), out_...  9.27 us
    reshape x2, local copies, waits for them, and re-layouts, per_device(): acts_deq = acts_deq.reshape(local_tokens, lanes, quarter).transpose(1, 0, 2)  6.45 us

profile of v1, /device:TPU:0, one launch (start us, length us, event | category | flops | bytes accessed | tf_op | source)
XLA Modules:
  0.0 171.3 jit_solution(10604244618777374562)
XLA Ops:
  0.6 0.7 convert_element_type.20
  1.3 0.1 broadcast_bitcast_fusion
  1.4 0.7 bitcast_convert_fusion
  2.1 2.1 %multiply_convert_fusion.1 = bf16[2,128,4096]{2,1,0:T(8,128)(2,1)S(1)} fusion(bf16[2,128,4096]{2,1,0:T(8,128)(2,1)} %param.7, f32[2,4096]{1,0:T(2,128)S(1)} %bitcast.36), kind=kLoop, calls=%fused_computation.15 | loop fusion | flops 3145728 | bytes 4227072 | tf_op jit(solution)/shard_map/convert_element_type | solution.py:287
  4.2 2.8 %reshape.30 = bf16[256,4,1024]{2,1,0:T(4,128)(2,1)} reshape(bf16[2,128,4096]{2,1,0:T(8,128)(2,1)S(1)} %multiply_convert_fusion.1) | data formatting | bytes 4194304 | tf_op jit(solution)/shard_map/reshape | solution.py:288
  7.0 3.7 %copy.31 = bf16[256,4,1024]{2,0,1:T(8,128)(2,1)} copy(bf16[256,4,1024]{2,1,0:T(4,128)(2,1)} %reshape.30) | data formatting | bytes 4194304 | tf_op jit(solution)/shard_map/reshape | solution.py:288
  10.7 0.0 copy-done.1
  10.7 0.6 multiply_convert_fusion
  11.2 0.5 copy.26
  11.7 1.8 %copy.30 = bf16[256,8,640]{2,0,1:T(8,128)(2,1)} copy(bf16[256,8,640]{2,1,0:T(8,128)(2,1)S(1)} %bitcast.34) | data formatting | bytes 5242880 | tf_op jit(solution)/shard_map/reshape | solution.py:290
  13.6 103.8 %shard_map.102 = (bf16[32,256,1024]{2,1,0:T(8,128)(2,1)}, bf16[8,256,640]{2,1,0:T(8,128)(2,1)}) custom-call(bf16[4,256,1024]{2,1,0:T(8,128)(2,1)} %bitcast.35, bf16[8,256,640]{2,1,0:T(8,128)(2,1)} %bitcast.32), custom_call_target="tpu_custom_call" | custom-call | tf_op jit(solution)/shard_map/pallas_call | solution.py:189
  117.4 0.0 slice-start
  117.4 0.0 slice-start.1
  117.4 6.0 %fusion.18 = f32[640,1024]{1,0:T(8,128)S(1)} fusion(bf16[8,256,640]{2,1,0:T(8,128)(2,1)} %get-tuple-element.6, bf16[32,256,1024]{2,1,0:T(8,128)(2,1)} %get-tuple-element.7), kind=kOutput, calls=%fused_computation.21 | convolution fusion | flops 2684354560 | bytes 9437184 | tf_op jit(solution)/shard_map/dot_general | solution.py:298
  123.4 0.0 slice-start.2
  123.4 0.0 slice-start.3
  123.4 4.9 %fusion.15 = f32[640,1024]{1,0:T(8,128)S(1)} fusion(bf16[8,256,640]{2,1,0:T(8,128)(2,1)S(1)} %copy-done.2, bf16[32,256,1024]{2,1,0:T(8,128)(2,1)} %get-tuple-element.7), kind=kOutput, calls=%fused_computation.20 | convolution fusion | flops 2684354560 | bytes 9437184 | tf_op jit(solution)/shard_map/dot_general | solution.py:298
  128.4 2.9 %fusion.12 = f32[640,1024]{1,0:T(8,128)S(1)} fusion(bf16[8,256,640]{2,1,0:T(8,128)(2,1)S(1)} %copy-done.2, bf16[32,256,1024]{2,1,0:T(8,128)(2,1)S(1)} %bitcast.38), kind=kOutput, calls=%fused_computation.19 | convolution fusion | flops 2684354560 | bytes 9437184 | tf_op jit(solution)/shard_map/dot_general | solution.py:298
  131.3 2.9 %fusion.9 = f32[640,1024]{1,0:T(8,128)S(1)} fusion(bf16[8,256,640]{2,1,0:T(8,128)(2,1)S(1)} %copy-done.2, bf16[32,256,1024]{2,1,0:T(8,128)(2,1)S(1)} %bitcast.38), kind=kOutput, calls=%fused_computation.18 | convolution fusion | flops 2684354560 | bytes 9437184 | tf_op jit(solution)/shard_map/dot_general | solution.py:298
  134.2 2.8 %bitcast_reduce_fusion.part = f32[8,128]{1,0:T(8,128)S(1)} fusion(f32[640,1024]{1,0:T(8,128)S(1)} %fusion.18, f32[640,1024]{1,0:T(8,128)S(1)} %fusion.15, f32[640,1024]{1,0:T(8,128)S(1)} %fusion.12, f32[640,1024]{1,0:T(8,128)S(1)} %fusion.9), kind=kLoop, calls=%fused_computation.3 | loop fusion | flops 13106176 | bytes 10489856 | tf_op jit(solution)/shard_map/reduce_sum | solution.py:303
  137.0 0.0 copy-done
  137.0 9.3 %shard_map.103 = f32[8,128]{1,0:T(8,128)S(1)} custom-call(f32[8,128]{1,0:T(8,128)S(1)} %bitcast_reduce_fusion.part), custom_call_target="tpu_custom_call" | custom-call | tf_op jit(solution)/shard_map/pallas_call | solution.py:258
  146.3 0.5 slice.23
  146.8 24.5 %fusion.21 = (bf16[640,4096]{1,0:T(8,128)(2,1)}, f32[640,4096]{1,0:T(8,128)}, f32[640,4096]{1,0:T(8,128)}, f32[640,4096]{1,0:T(8,128)}) fusion(f32[640,4096]{1,0:T(8,128)} %param.13, f32[640,1024]{1,0:T(8,128)S(1)} %fusion.18, f32[640,1024]{1,0:T(8,128)S(1)} %fusion.15, f32[640,1024]{1,0:T(8,128)S(1)} %fusion.12, f32[640,1024]{1,0:T(8,128)} %copy-done, ...), kind=kLoop, calls=%fused_computation.25 | loop fusion | flops 41943040 | bytes 78643200 | tf_op jit(solution)/shard_map/convert_element_type | solution.py:310
  (10 shorter events, 0.0 us)
Async XLA Ops:
  7.0 3.7 %copy-start.1 = (bf16[2,128,5120]{2,1,0:T(8,128)(2,1)S(1)}, bf16[2,128,5120]{2,1,0:T(8,128)(2,1)}, u32[]{:S(2)}) copy-start(bf16[2,128,5120]{2,1,0:T(8,128)(2,1)} %param.8) | copy-start | bytes 7864324
  117.4 6.0 %copy-start.2 = (bf16[8,256,640]{2,1,0:T(8,128)(2,1)S(1)}, bf16[8,256,640]{2,1,0:T(8,128)(2,1)}, u32[]{:S(2)}) copy-start(bf16[8,256,640]{2,1,0:T(8,128)(2,1)} %get-tuple-element.6) | copy-start | bytes 7864324
  117.4 10.9 %slice-start = ((s8[16777216]{0:T(1024)(128)(4,1)}), s8[4194304]{0:T(1024)(128)(4,1)S(1)}, s32[]{:S(2)}) async-start(s8[16777216]{0:T(1024)(128)(4,1)} %bitcast.37), calls=%async_computation | async-start | bytes 8388608
  117.4 10.9 %slice-start.1 = ((s8[16777216]{0:T(1024)(128)(4,1)}), s8[4194304]{0:T(1024)(128)(4,1)S(1)}, s32[]{:S(2)}) async-start(s8[16777216]{0:T(1024)(128)(4,1)} %bitcast.37), calls=%async_computation.1 | async-start | bytes 8388608
  123.4 4.9 %slice-start.2 = ((s8[16777216]{0:T(1024)(128)(4,1)}), s8[4194304]{0:T(1024)(128)(4,1)S(1)}, s32[]{:S(2)}) async-start(s8[16777216]{0:T(1024)(128)(4,1)} %bitcast.37), calls=%async_computation.2 | async-start | bytes 8388608
  123.4 4.9 %slice-start.3 = ((s8[16777216]{0:T(1024)(128)(4,1)}), s8[4194304]{0:T(1024)(128)(4,1)S(1)}, s32[]{:S(2)}) async-start(s8[16777216]{0:T(1024)(128)(4,1)} %bitcast.37), calls=%async_computation.3 | async-start | bytes 8388608
  134.2 2.8 %copy-start = (f32[640,1024]{1,0:T(8,128)}, f32[640,1024]{1,0:T(8,128)S(1)}, u32[]{:S(2)}) copy-start(f32[640,1024]{1,0:T(8,128)S(1)} %fusion.9) | copy-start | bytes 7864324

commit v2 on v1

--- a/solution.py
+++ b/solution.py
@@ -271,6 +271,29 @@
     )(part)
 
 
+def scale_kernel(x, scale, out):
+    out[0] = (x[0].astype(jnp.float32) * scale[0].astype(jnp.float32)).astype(out.dtype)
+
+
+def scaled_pieces(x, scale, pieces):
+    blocks, tokens, columns = x.shape
+    width = columns // pieces
+    if width % 128:
+        whole = (x.astype(jnp.float32) * scale.astype(jnp.float32)).astype(jnp.bfloat16)
+        return whole.reshape(blocks * tokens, pieces, width).transpose(1, 0, 2)
+    return pl.pallas_call(
+        scale_kernel,
+        grid=(pieces, blocks),
+        out_shape=jax.ShapeDtypeStruct((pieces, blocks * tokens, width), jnp.bfloat16),
+        in_specs=[
+            pl.BlockSpec((1, tokens, width), lambda p, b: (b, 0, p)),
+            pl.BlockSpec((1, 1, width), lambda p, b: (b, 0, p)),
+        ],
+        out_specs=pl.BlockSpec((1, tokens, width), lambda p, b: (p, b, 0)),
+        compiler_params=pltpu.CompilerParams(vmem_limit_bytes=8 * 1024 * 1024),
+    )(x, scale)
+
+
 def per_device(activations, out_grads, act_scale, grad_scale, moment, second, master):
     owners = lax.axis_size("dp")
     lanes = lax.axis_size("tensor")
@@ -284,10 +307,8 @@
     spread = jnp.broadcast_to(
         act_scale.astype(jnp.float32)[:, :, None], (blocks, tiles, weight_rows // tiles)
     ).reshape(blocks, 1, weight_rows)
-    acts_deq = (activations.astype(jnp.float32) * spread).astype(jnp.bfloat16)
-    acts_deq = acts_deq.reshape(local_tokens, lanes, quarter).transpose(1, 0, 2)
-    grads_deq = (out_grads.astype(jnp.float32) * grad_scale.astype(jnp.float32)).astype(jnp.bfloat16)
-    grads_deq = grads_deq.reshape(local_tokens, owners, owned).transpose(1, 0, 2)
+    acts_deq = scaled_pieces(activations, spread, lanes)
+    grads_deq = scaled_pieces(out_grads, grad_scale, owners)
     piece, moved = gather_all(acts_deq, grads_deq, owners)
     total = owners * local_tokens
     moved = moved.reshape(total, owned)

time: 172 us -> 168 us (0.977)
  other arithmetic: 31.3 us -> 27.2 us
  Pallas kernels: 113 us -> 115 us
    reshape x3 -> x0, local copies, waits for them, and re-layouts: 8.27 us -> none  [the longest x2 6.45 us: per_device(): acts_deq = acts_deq.reshape(local_tokens, lanes, quarter).transpose(1, 0, 2)]
    unnamed x17 -> x21, local copies, waits for them, and re-layouts: 0.62 us -> 6.92 us
    convert_element_type x3 -> x0, other arithmetic: 3.29 us -> none  [the longest x1 2.06 us: per_device(): acts_deq = (activations.astype(jnp.float32) * spread).astype(jnp.bfloat16)]
    pallas_call x0 -> x2, Pallas kernels: none -> 1.85 us  [scaled_pieces(): pl.pallas_call(scale_kernel, grid=(pieces, blocks), out_shape=jax.ShapeDt...]
where the time goes in v2:
time: 168 us
  Pallas kernels  115 us (68%)
  other arithmetic  27.2 us (16%)
  matrix products  16.7 us (10%)
  local copies, waits for them, and re-layouts  8.12 us (5%)
    pallas_call x1, Pallas kernels, gather_all(): pl.pallas_call(functools.partial(gather_kernel, owners, lanes), out_shape...  104 us
    convert_element_type x1, other arithmetic, per_device(): weights = new_master.astype(jnp.bfloat16)  24.4 us
    dot_general x4, matrix products, per_device(): lax.dot_general(moved, piece[t], (((0,), (0,)), ((), ())), preferred_elem...  16.7 us
    pallas_call x1, Pallas kernels, clip_factor(): pl.pallas_call(functools.partial(norm_kernel, owners, lanes, limit), out_...  9.26 us
    unnamed x21, local copies, waits for them, and re-layouts  6.92 us

profile of v2, /device:TPU:0, one launch (start us, length us, event | category | flops | bytes accessed | tf_op | source)
XLA Modules:
  0.0 167.8 jit_solution(6491881553245202939)
XLA Ops:
  0.6 0.7 broadcast_in_dim.2
  1.4 0.8 copy.11.scale
  2.1 0.0 copy-start.3
  2.1 1.6 copy-done.3
  3.7 0.7 shard_map.102.acts
  4.4 0.0 copy-start.1
  4.4 1.3 copy-done.1
  5.7 1.7 %copy-done.2 = bf16[2,128,5120]{2,1,0:T(8,128)(2,1)S(1)} copy-done((bf16[2,128,5120]{2,1,0:T(8,128)(2,1)S(1)}, bf16[2,128,5120]{2,1,0:T(8,128)(2,1)}, u32[]{:S(2)}) %copy-start.2) | copy-done | bytes 2621464
  7.5 1.2 shard_map.103.grads
  8.6 0.0 copy-start
  8.7 1.5 copy-done
  10.1 103.8 %shard_map.104 = (bf16[32,256,1024]{2,1,0:T(8,128)(2,1)}, bf16[8,256,640]{2,1,0:T(8,128)(2,1)}) custom-call(bf16[4,256,1024]{2,1,0:T(8,128)(2,1)} %copy-done.1, bf16[8,256,640]{2,1,0:T(8,128)(2,1)} %copy-done), custom_call_target="tpu_custom_call" | custom-call | tf_op jit(solution)/shard_map/pallas_call | solution.py:189
  113.9 0.0 slice-start
  114.0 0.0 slice-start.1
  114.0 6.0 %fusion.18 = f32[640,1024]{1,0:T(8,128)S(1)} fusion(bf16[8,256,640]{2,1,0:T(8,128)(2,1)} %get-tuple-element.6, bf16[32,256,1024]{2,1,0:T(8,128)(2,1)} %get-tuple-element.7), kind=kOutput, calls=%fused_computation.17 | convolution fusion | flops 2684354560 | bytes 9437184 | tf_op jit(solution)/shard_map/dot_general | solution.py:319
  119.9 0.0 slice-start.2
  119.9 0.0 slice-start.3
  120.0 4.9 %fusion.15 = f32[640,1024]{1,0:T(8,128)S(1)} fusion(bf16[8,256,640]{2,1,0:T(8,128)(2,1)S(1)} %copy-done.5, bf16[32,256,1024]{2,1,0:T(8,128)(2,1)} %get-tuple-element.7), kind=kOutput, calls=%fused_computation.16 | convolution fusion | flops 2684354560 | bytes 9437184 | tf_op jit(solution)/shard_map/dot_general | solution.py:319
  124.9 2.9 %fusion.12 = f32[640,1024]{1,0:T(8,128)S(1)} fusion(bf16[8,256,640]{2,1,0:T(8,128)(2,1)S(1)} %copy-done.5, bf16[32,256,1024]{2,1,0:T(8,128)(2,1)S(1)} %bitcast.18), kind=kOutput, calls=%fused_computation.15 | convolution fusion | flops 2684354560 | bytes 9437184 | tf_op jit(solution)/shard_map/dot_general | solution.py:319
  127.8 2.9 %fusion.9 = f32[640,1024]{1,0:T(8,128)S(1)} fusion(bf16[8,256,640]{2,1,0:T(8,128)(2,1)S(1)} %copy-done.5, bf16[32,256,1024]{2,1,0:T(8,128)(2,1)S(1)} %bitcast.18), kind=kOutput, calls=%fused_computation.14 | convolution fusion | flops 2684354560 | bytes 9437184 | tf_op jit(solution)/shard_map/dot_general | solution.py:319
  130.8 2.8 %bitcast_reduce_fusion.part = f32[8,128]{1,0:T(8,128)S(1)} fusion(f32[640,1024]{1,0:T(8,128)S(1)} %fusion.18, f32[640,1024]{1,0:T(8,128)S(1)} %fusion.15, f32[640,1024]{1,0:T(8,128)S(1)} %fusion.12, f32[640,1024]{1,0:T(8,128)S(1)} %fusion.9), kind=kLoop, calls=%fused_computation.3 | loop fusion | flops 13106176 | bytes 10489856 | tf_op jit(solution)/shard_map/reduce_sum | solution.py:324
  133.6 9.3 %shard_map.105 = f32[8,128]{1,0:T(8,128)S(1)} custom-call(f32[8,128]{1,0:T(8,128)S(1)} %bitcast_reduce_fusion.part), custom_call_target="tpu_custom_call" | custom-call | tf_op jit(solution)/shard_map/pallas_call | solution.py:258
  142.8 0.5 slice.23
  143.3 24.4 %fusion.21 = (bf16[640,4096]{1,0:T(8,128)(2,1)}, f32[640,4096]{1,0:T(8,128)}, f32[640,4096]{1,0:T(8,128)}, f32[640,4096]{1,0:T(8,128)}) fusion(f32[640,4096]{1,0:T(8,128)} %param.13, f32[640,1024]{1,0:T(8,128)S(1)} %fusion.18, f32[640,1024]{1,0:T(8,128)S(1)} %fusion.15, f32[640,1024]{1,0:T(8,128)S(1)} %fusion.12, f32[640,1024]{1,0:T(8,128)} %copy-done.4, ...), kind=kLoop, calls=%fused_computation.18 | loop fusion | flops 41943040 | bytes 78643200 | tf_op jit(solution)/shard_map/convert_element_type | solution.py:331
  (10 shorter events, 0.0 us)
Async XLA Ops:
  2.1 1.6 copy-start.3
  4.4 1.3 copy-start.1
  5.7 1.7 %copy-start.2 = (bf16[2,128,5120]{2,1,0:T(8,128)(2,1)S(1)}, bf16[2,128,5120]{2,1,0:T(8,128)(2,1)}, u32[]{:S(2)}) copy-start(bf16[2,128,5120]{2,1,0:T(8,128)(2,1)} %x.3) | copy-start | bytes 7864324
  8.6 1.5 copy-start
  113.9 6.0 %copy-start.5 = (bf16[8,256,640]{2,1,0:T(8,128)(2,1)S(1)}, bf16[8,256,640]{2,1,0:T(8,128)(2,1)}, u32[]{:S(2)}) copy-start(bf16[8,256,640]{2,1,0:T(8,128)(2,1)} %get-tuple-element.6) | copy-start | bytes 7864324
  113.9 10.9 %slice-start = ((s8[16777216]{0:T(1024)(128)(4,1)}), s8[4194304]{0:T(1024)(128)(4,1)S(1)}, s32[]{:S(2)}) async-start(s8[16777216]{0:T(1024)(128)(4,1)} %bitcast.17), calls=%async_computation | async-start | bytes 8388608
  114.0 10.9 %slice-start.1 = ((s8[16777216]{0:T(1024)(128)(4,1)}), s8[4194304]{0:T(1024)(128)(4,1)S(1)}, s32[]{:S(2)}) async-start(s8[16777216]{0:T(1024)(128)(4,1)} %bitcast.17), calls=%async_computation.1 | async-start | bytes 8388608
  119.9 4.9 %slice-start.2 = ((s8[16777216]{0:T(1024)(128)(4,1)}), s8[4194304]{0:T(1024)(128)(4,1)S(1)}, s32[]{:S(2)}) async-start(s8[16777216]{0:T(1024)(128)(4,1)} %bitcast.17), calls=%async_computation.2 | async-start | bytes 8388608
  119.9 4.9 %slice-start.3 = ((s8[16777216]{0:T(1024)(128)(4,1)}), s8[4194304]{0:T(1024)(128)(4,1)S(1)}, s32[]{:S(2)}) async-start(s8[16777216]{0:T(1024)(128)(4,1)} %bitcast.17), calls=%async_computation.3 | async-start | bytes 8388608
  130.8 12.5 %copy-start.4 = (f32[640,1024]{1,0:T(8,128)}, f32[640,1024]{1,0:T(8,128)S(1)}, u32[]{:S(2)}) copy-start(f32[640,1024]{1,0:T(8,128)S(1)} %fusion.9) | copy-start | bytes 7864324
